TPU v7x, 32 devices: a whole 2x2x4 slice. The times are simulated.
32 devices in a mesh: slab: 16 (over z, x, core), layer: 2 (over y).
Axes of the slice: x: 2, y: 2, z: 4, core: 2. Of those that a mesh axis runs over, the one named last changes fastest.
Arguments:
- nodal_field: float32 [2, 1024, 4, 4, 512], P('layer', 'slab'), may hold values from -6 to 6
- metric: float32 [2, 1024, 4, 4, 3, 512], P('layer', 'slab'), may hold values from 0.25 to 2
- slab_ids: int32 [1024], replicated, may hold values from 0 to 1023, as said below
- face_map: int32 [1024, 1024], P('slab'), may hold values from 0 to 1023, as said below
Outputs:
- assembled: float32 [2, 1024, 4, 4, 512], P('layer', 'slab')
Inputs may be any that keep to these rules, and one draw needn't show every extreme that they name: slab_ids is a permutation of 0 to 1023; positions p of one device are those with p // 64 equal to its index along slab, and for one rotation R every device holds exactly the slabs g with (g + R) mod 16 equal to its index, in any order of its positions, so slab (g + 1) mod 1024 always sits on the next device along slab, cyclically. Each row of face_map is a permutation of 0 to 1023: either the identity, or the map that reverses y, sending (ez, ey, c, b) to (ez, 3 - ey, c, 7 - b); z order is never changed.
All inputs are finite; a program needn't handle non-finite values.
Results may differ from a plain program's by a relative error of at most 0.00005.
Values sent between devices are 32-bit elements; how exact they have to be, the bound alone decides.
A program may use at most 192 MiB of HBM per device.

v0:
```python
import functools

import jax
import jax.numpy as jnp
import numpy as np
from jax import lax
from jax.experimental import pallas as pl
from jax.experimental.pallas import tpu as pltpu
from jax.sharding import PartitionSpec as P

P_SIZE = 8
PTS = 512
EY = 4
EZ = 4
SUB = 8
LANES = 128
SB = 8
SBF = 16


def legendre_pair(nodes, degree):
    lower = nodes * 0.0 + 1.0
    upper = nodes.copy()
    for order in range(2, degree + 1):
        lower, upper = upper, ((2 * order - 1) * nodes * upper - (order - 1) * lower) / order
    return lower, upper


def gll_tables():
    degree = P_SIZE - 1
    nodes = -np.cos(np.pi * np.arange(P_SIZE) / degree)
    for _ in range(100):
        lower, upper = legendre_pair(nodes, degree)
        nodes = nodes - (nodes * upper - lower) / ((degree + 1) * upper)
    lower, upper = legendre_pair(nodes, degree)
    rho = 2.0 / (degree * (degree + 1) * upper * upper)
    eye = np.eye(P_SIZE)
    differ = nodes[:, None] - nodes[None, :] + eye
    der = upper[:, None] / (upper[None, :] * differ) * (1.0 - eye)
    der[0, 0] = -degree * (degree + 1) / 4.0
    der[degree, degree] = degree * (degree + 1) / 4.0
    return der, rho


def two_parts(table):
    high = np.asarray(table, np.float32).astype(jnp.bfloat16)
    low = (table - high.astype(np.float64)).astype(jnp.bfloat16)
    return high, low


def tables():
    der, rho = gll_tables()
    eye8, eye2 = np.eye(8), np.eye(2)
    plane = np.tile(np.kron(rho, rho), 2)
    fwd = np.concatenate(
        [np.kron(np.eye(16), der.T) * plane, np.kron(eye2, np.kron(der.T, eye8)) * plane], 1
    )
    high, low = two_parts(fwd)
    fwd_op = np.concatenate([high, high, low], 0)
    bwd = np.concatenate([np.kron(np.eye(16), der), np.kron(eye2, np.kron(der, eye8))], 0)
    high, low = two_parts(bwd)
    half = np.concatenate([high, low], 1)
    bwd_op = np.concatenate([half, half], 0)
    l2 = (np.arange(SUB) // EY)[:, None]
    h = (np.arange(LANES) // 64)[None, :]
    cube_plane = plane[None, :]
    zf = np.zeros((2, 2, 2, 2, SUB, LANES))
    zb = np.zeros((2, 2, 2, 2, SUB, LANES))
    rc = np.zeros((2, SUB, LANES))
    for lo in range(2):
        c_out = 2 * (2 * lo + l2) + h
        rc[lo] = rho[c_out]
        for li in range(2):
            for s in range(2):
                for l in range(2):
                    c_in = 2 * (2 * li + (l2 ^ s)) + (h ^ l)
                    zf[lo, l, li, s] = np.roll(der[c_out, c_in] * rho[c_out] * cube_plane, 64 * l, 1)
                    zb[lo, l, li, s] = np.roll(der[c_in, c_out], 64 * l, 1)
    consts = np.concatenate([zf.reshape(-1, SUB, LANES), zb.reshape(-1, SUB, LANES), rc], 0)
    return fwd_op, bwd_op, consts.astype(np.float32)


def roll_sub(x, by):
    return pltpu.roll(x, by % SUB, axis=x.ndim - 2)


def roll_lane(x, by):
    return pltpu.roll(x, by % LANES, axis=x.ndim - 1)


def split(x):
    high = x.astype(jnp.bfloat16)
    return high, (x - high.astype(jnp.float32)).astype(jnp.bfloat16)


def iotas():
    sub = lax.broadcasted_iota(jnp.int32, (SUB, LANES), 0)
    lane = lax.broadcasted_iota(jnp.int32, (SUB, LANES), 1)
    return sub, lane


def lane_gather(x, index):
    return jnp.take_along_axis(x, index, axis=1, mode="promise_in_bounds")


def flip(x, sub, lane):
    y = lane_gather(x, lane ^ 7)
    e = sub % EY
    return jnp.where(
        e == 0, roll_sub(y, -3), jnp.where(e == 1, roll_sub(y, -1), jnp.where(e == 2, roll_sub(y, 1), roll_sub(y, 3)))
    )


def apply_z(pair, consts, base):
    terms = []
    for v in pair:
        terms += [v, roll_sub(v, 4)]
    out = []
    for lo in range(2):
        near, far = (
            sum_of([consts[base + 8 * lo + 4 * half + t] * terms[t] for t in range(4)])
            for half in range(2)
        )
        out.append(near + roll_lane(far, 64))
    return out


def sum_of(parts):
    return (parts[0] + parts[1]) + (parts[2] + parts[3])


def slab_work(sb, u_ref, m_ref, fm_ref, fwd_ref, bwd_ref, consts, put_v, put_faces):
    rows = sb * 64
    u = u_ref[...]
    high, low = split(u)
    g = jnp.dot(
        jnp.concatenate([high, low, high], 1), fwd_ref[...], preferred_element_type=jnp.float32
    )
    m = m_ref[...].reshape(sb * EZ, 3, 16, LANES)
    gx = g[:, :LANES].reshape(sb * EZ, 16, LANES)
    gy = g[:, LANES:].reshape(sb * EZ, 16, LANES)
    fx = (gx * m[:, 0]).reshape(rows, LANES)
    fy = (gy * m[:, 1]).reshape(rows, LANES)
    xh, xl = split(fx)
    yh, yl = split(fy)
    r = jnp.dot(
        jnp.concatenate([xh, yh, xl, yl], 1), bwd_ref[...], preferred_element_type=jnp.float32
    )
    r = (r[:, :LANES] + r[:, LANES:]).reshape(sb * EZ, 2, SUB, LANES)
    u4 = u.reshape(sb * EZ, 2, SUB, LANES)
    mz = m[:, 2].reshape(sb * EZ, 2, SUB, LANES)
    sub, lane = iotas()
    ey, b = sub % EY, lane // 8 % 8
    mask_up = (ey < EY - 1) & (b == 7)
    mask_dn = (ey > 0) & (b == 0)
    top_mask = (sub >= 4) & (lane >= 64)
    bot_mask = (sub < 4) & (lane < 64)
    group = lane // 16 % 4
    pick = (lane % 16) * 8 + 7 * (lane // 64)
    edges = [None, None]
    z_hold = None
    for s in range(sb):
        v = []
        for ez in range(EZ):
            i = s * EZ + ez
            gz = apply_z([u4[i, 0], u4[i, 1]], consts, 0)
            out = apply_z([gz[0] * mz[i, 0], gz[1] * mz[i, 1]], consts, 16)
            for t in range(2):
                w = out[t] + consts[32 + t] * r[i, t]
                up = roll_lane(roll_sub(w, -1), 56)
                dn = roll_lane(roll_sub(w, 1), -56)
                v.append(w + jnp.where(mask_up, up, 0.0) + jnp.where(mask_dn, dn, 0.0))
        for ez in range(EZ - 1):
            a, c = v[2 * ez + 1], v[2 * ez + 2]
            v[2 * ez + 1] = a + jnp.where(top_mask, roll_lane(roll_sub(c, 4), 64), 0.0)
            v[2 * ez + 2] = c + jnp.where(bot_mask, roll_lane(roll_sub(a, 4), 64), 0.0)
        packs = []
        for k in range(8):
            put_v(s, k, v[k])
            got = lane_gather(v[k], pick)
            if k % 4 == 0:
                packs.append(got)
            else:
                packs[-1] = jnp.where(group == k % 4, got, packs[-1])
        low_half = lane < 64
        left = jnp.where(low_half, packs[0], roll_lane(packs[1], 64))
        right = jnp.where(low_half, roll_lane(packs[0], 64), packs[1])
        flag = jnp.broadcast_to(fm_ref[s : s + 1, 0:1], (SUB, LANES)) != 0
        right = jnp.where(flag, flip(right, sub, lane), right)
        put_faces(0, s, right)
        put_faces(1, s, left)
        for side, face in enumerate((right, left)):
            edge = roll_sub(jnp.where(sub < 4, face, roll_lane(face, 8)), 4)
            edge = roll_lane(edge, 8 * s) if s else edge
            edges[side] = edge if s == 0 else jnp.where(lane // 8 == s, edge, edges[side])
        z = jnp.where(sub < 4, v[0], v[7])
        if s % 2 == 0:
            z_hold = z
        else:
            put_faces(2, s // 2, jnp.where((sub < 4) == (lane < 64), z_hold, roll_lane(z, 64)))
    put_faces(3, 0, edges[0])
    put_faces(4, 0, edges[1])


def local_kernel(
    sb, steps, peers, u_ref, m_ref, fm_ref, fwd_ref, bwd_ref, consts,
    v_ref, *refs
):
    landing, sending, (send_sem, recv_sem) = refs[:5], refs[5:10], refs[10:]
    step = pl.program_id(0)
    me, layer = lax.axis_index("slab"), lax.axis_index("layer")
    right, left = lax.rem(me + 1, peers), lax.rem(me + peers - 1, peers)
    targets = (
        {"slab": right, "layer": layer},
        {"slab": left, "layer": layer},
        {"slab": me, "layer": 1 - layer},
        {"slab": right, "layer": 1 - layer},
        {"slab": left, "layer": 1 - layer},
    )
    sizes = (sb, sb, sb // 2, 1, 1)
    barrier = pltpu.get_barrier_semaphore()

    def copy_of(which, at):
        rows = pl.ds(at * sizes[which], sizes[which])
        return pltpu.make_async_remote_copy(
            src_ref=sending[which].at[rows],
            dst_ref=landing[which].at[rows],
            send_sem=send_sem.at[which, at],
            recv_sem=recv_sem.at[which, at],
            device_id=targets[which],
            device_id_type=pl.DeviceIdType.MESH,
        )

    @pl.when(step == 0)
    def _():
        for target in targets:
            pl.semaphore_signal(
                barrier, inc=1, device_id=target, device_id_type=pl.DeviceIdType.MESH
            )

    @pl.when(step == 1)
    def _():
        pl.semaphore_wait(barrier, 5)

    @pl.when(step > 0)
    def _():
        for which in range(5):
            copy_of(which, step - 1).start()

    def put_v(s, k, value):
        v_ref[pl.ds(s * 64 + k * 8, 8), :] = value

    def put_faces(which, at, value):
        sending[which][step * sizes[which] + at] = value

    slab_work(sb, u_ref, m_ref, fm_ref, fwd_ref, bwd_ref, consts, put_v, put_faces)

    @pl.when(step == steps - 1)
    def _():
        def drain(at, carry):
            for which in range(5):
                copy_of(which, at).wait_send()
            return carry

        def collect(at, carry):
            for which in range(5):
                copy_of(which, at).wait_recv()
            return carry

        lax.fori_loop(0, steps - 2, drain, 0)
        for which in range(5):
            copy_of(which, steps - 1).start()
        drain(steps - 2, 0)
        drain(steps - 1, 0)
        lax.fori_loop(0, steps, collect, 0)


def finish_kernel(
    sb, per_edge, slabs, peers, ids_ref, v_ref, fm_ref, pr_ref, pl_ref, z_ref, er_ref, el_ref, out_ref, inv_ref
):
    step = pl.program_id(0)
    me = lax.axis_index("slab")
    total = slabs * peers
    behind = lax.rem(me + peers - 1, peers) * slabs
    ahead = lax.rem(me + 1, peers) * slabs

    @pl.when(step == 0)
    def _():
        for p in range(slabs):
            inv_ref[0, lax.div(ids_ref[behind + p], peers)] = p
            inv_ref[1, lax.div(ids_ref[ahead + p], peers)] = p

    sub, lane = iotas()
    top_mask = (sub >= 4) & (lane >= 64)
    bot_mask = (sub < 4) & (lane < 64)
    a = lane % 8
    on_face = (a == 0) | (a == 7)
    spread = lane // 8 + 64 * (a == 7).astype(jnp.int32)

    def edge_of(ref, q):
        e = pltpu.roll(ref[lax.div(q, per_edge)], LANES - 8 * lax.rem(q, per_edge), axis=1)
        return jnp.where(
            (sub < 4) & (lane < 8), e, jnp.where((sub >= 4) & (lane >= 120), roll_lane(e, -8), 0.0)
        )

    packs = []
    for s in range(sb):
        own = ids_ref[me * slabs + step * sb + s]
        q_prev = inv_ref[0, lax.div(lax.rem(own + total - 1, total), peers)]
        q_next = inv_ref[1, lax.div(lax.rem(own + 1, total), peers)]
        left = pr_ref[q_prev] + edge_of(er_ref, q_prev)
        right = pl_ref[q_next] + edge_of(el_ref, q_next)
        flag = jnp.broadcast_to(fm_ref[s : s + 1, 0:1], (SUB, LANES)) != 0
        right = jnp.where(flag, flip(right, sub, lane), right)
        z = z_ref[s // 2]
        if s % 2:
            z = roll_lane(z, 64)
        z = roll_lane(roll_sub(z, 4), 64)
        low_half = lane < 64
        packs.append(
            (
                jnp.where(low_half, left, roll_lane(right, 64)),
                jnp.where(low_half, roll_lane(left, 64), right),
                z,
            )
        )
    for k in range(8):
        for s in range(sb):
            w = v_ref[pl.ds(s * 64 + k * 8, 8), :]
            w = w + jnp.where(on_face, lane_gather(packs[s][k // 4], spread + 16 * (k % 4)), 0.0)
            if k == 0:
                w = w + jnp.where(bot_mask, packs[s][2], 0.0)
            if k == 7:
                w = w + jnp.where(top_mask, packs[s][2], 0.0)
            out_ref[pl.ds(s * 64 + k * 8, 8), :] = w


def body(sb, sbf, peers, nodal_field, metric, slab_ids, face_map):
    slabs = nodal_field.shape[1]
    steps = slabs // sb
    fwd_op, bwd_op, consts = tables()
    u = nodal_field.reshape(slabs, EZ, EY, 4, LANES).transpose(0, 1, 3, 2, 4).reshape(slabs * 64, LANES)
    m = (
        metric.reshape(slabs, EZ, EY, 3, 4, LANES)
        .transpose(0, 1, 3, 4, 2, 5)
        .reshape(slabs * 192, LANES)
    )
    f32 = jnp.float32
    whole = lambda shape: pl.BlockSpec(shape, lambda i: (0,) * len(shape))
    stack = lambda n: pl.BlockSpec((n, SUB, LANES), lambda i: (i, 0, 0))
    v, pr, plf, z, er, el = pl.pallas_call(
        functools.partial(local_kernel, sb, steps, peers),
        grid=(steps,),
        in_specs=[
            pl.BlockSpec((sb * 64, LANES), lambda i: (i, 0)),
            pl.BlockSpec((sb * 192, LANES), lambda i: (i, 0)),
            pl.BlockSpec((sb, LANES), lambda i: (i, 0)),
            whole(fwd_op.shape),
            whole(bwd_op.shape),
            whole(consts.shape),
        ],
        out_specs=[
            pl.BlockSpec((sb * 64, LANES), lambda i: (i, 0)),
            *[pl.BlockSpec(memory_space=pl.ANY)] * 5,
        ],
        out_shape=[
            jax.ShapeDtypeStruct((slabs * 64, LANES), f32),
            jax.ShapeDtypeStruct((slabs, SUB, LANES), f32),
            jax.ShapeDtypeStruct((slabs, SUB, LANES), f32),
            jax.ShapeDtypeStruct((slabs // 2, SUB, LANES), f32),
            jax.ShapeDtypeStruct((steps, SUB, LANES), f32),
            jax.ShapeDtypeStruct((steps, SUB, LANES), f32),
        ],
        scratch_shapes=[
            pltpu.VMEM((slabs, SUB, LANES), f32),
            pltpu.VMEM((slabs, SUB, LANES), f32),
            pltpu.VMEM((slabs // 2, SUB, LANES), f32),
            pltpu.VMEM((steps, SUB, LANES), f32),
            pltpu.VMEM((steps, SUB, LANES), f32),
            pltpu.SemaphoreType.DMA((5, steps)),
            pltpu.SemaphoreType.DMA((5, steps)),
        ],
        compiler_params=pltpu.CompilerParams(collective_id=0, has_side_effects=True),
        name="local",
    )(u, m, face_map, jnp.asarray(fwd_op), jnp.asarray(bwd_op), jnp.asarray(consts))
    out = pl.pallas_call(
        functools.partial(finish_kernel, sbf, sb, slabs, peers),
        grid=(slabs // sbf,),
        in_specs=[
            pl.BlockSpec(memory_space=pltpu.SMEM),
            pl.BlockSpec((sbf * 64, LANES), lambda i: (i, 0)),
            pl.BlockSpec((sbf, LANES), lambda i: (i, 0)),
            whole((slabs, SUB, LANES)),
            whole((slabs, SUB, LANES)),
            stack(sbf // 2),
            whole((steps, SUB, LANES)),
            whole((steps, SUB, LANES)),
        ],
        out_specs=pl.BlockSpec((sbf * 64, LANES), lambda i: (i, 0)),
        out_shape=jax.ShapeDtypeStruct((slabs * 64, LANES), f32),
        scratch_shapes=[pltpu.SMEM((2, slabs), jnp.int32)],
        name="finish",
    )(slab_ids, v, face_map, pr, plf, z, er, el)
    out = out.reshape(slabs, EZ, 4, EY, LANES).transpose(0, 1, 3, 2, 4)
    return out.reshape(1, slabs, EZ, EY, PTS)


def solution(mesh):
    return jax.shard_map(
        functools.partial(body, SB, SBF, mesh.shape["slab"]),
        mesh=mesh,
        in_specs=(
            P("layer", "slab", None, None, None),
            P("layer", "slab", None, None, None, None),
            P(),
            P("slab", None),
        ),
        out_specs=P("layer", "slab", None, None, None),
        check_vma=False,
    )
```

profile of v0, /device:TPU:0, one launch (start us, length us, event | category | flops | bytes accessed | tf_op | source)
XLA Modules:
  0.0 27.9 jit_solution(1992606493609451441)
XLA Ops:
  0.0 21.6 %local.1 = (f32[4096,128]{1,0:T(8,128)}, f32[64,8,128]{2,1,0:T(8,128)}, f32[64,8,128]{2,1,0:T(8,128)}, f32[32,8,128]{2,1,0:T(8,128)}, f32[8,8,128]{2,1,0:T(8,128)}, /*index=5*/f32[8,8,128]{2,1,0:T(8,128)}) custom-call(f32[4096,128]{1,0:T(8,128)} %bitcast.16, f32[12288,128]{1,0:T(8,128)} %bitcast.15, s32[64,1024]{1,0:T(8,128)} %fm_ref.3, ...), custom_call_target="tpu_custom_call" | custom-call | tf_op jit(solution)/shard_map/local/pallas_call | solution.py:351
  21.6 6.3 %finish.1 = f32[4096,128]{1,0:T(8,128)} custom-call(s32[1024]{0:T(1024)} %ids_ref.1, f32[4096,128]{1,0:T(8,128)} %get-tuple-element.11.v_ref, s32[64,1024]{1,0:T(8,128)} %fm_ref.3, f32[64,8,128]{2,1,0:T(8,128)} %get-tuple-element.12.pr_ref, f32[64,8,128]{2,1,0:T(8,128)} %get-tuple-element.13.pl_ref, f32[32,8,128]{2,1,0:T(8,128)} %get-tuple-element.14.z_ref, ...), custom_call_target="tpu_custom_call" | custom-call | tf_op jit(solution)/shard_map/finish/pallas_call | solution.py:386
where the time goes:
time: 28.2 us; the launch traced here: 27.9 us
  Pallas kernels  27.9 us (99%)
    pallas_call x1, Pallas kernels, body(): pl.pallas_call(functools.partial(local_kernel, sb, steps, peers), grid=(s...  21.6 us
    pallas_call x1, Pallas kernels, body(): pl.pallas_call(functools.partial(finish_kernel, sbf, sb, slabs, peers), g...  6.26 us

commit v1 on v0

v1 whole, which is shorter than its diff:
```python
import functools

import jax
import jax.numpy as jnp
import numpy as np
from jax import lax
from jax.experimental import pallas as pl
from jax.experimental.pallas import tpu as pltpu
from jax.sharding import PartitionSpec as P

P_SIZE = 8
PTS = 512
EY = 4
EZ = 4
SUB = 8
LANES = 128
SB = 8
DEPTH = 3
GROUP = 16


def legendre_pair(nodes, degree):
    lower = nodes * 0.0 + 1.0
    upper = nodes.copy()
    for order in range(2, degree + 1):
        lower, upper = upper, ((2 * order - 1) * nodes * upper - (order - 1) * lower) / order
    return lower, upper


def gll_tables():
    degree = P_SIZE - 1
    nodes = -np.cos(np.pi * np.arange(P_SIZE) / degree)
    for _ in range(100):
        lower, upper = legendre_pair(nodes, degree)
        nodes = nodes - (nodes * upper - lower) / ((degree + 1) * upper)
    lower, upper = legendre_pair(nodes, degree)
    rho = 2.0 / (degree * (degree + 1) * upper * upper)
    eye = np.eye(P_SIZE)
    differ = nodes[:, None] - nodes[None, :] + eye
    der = upper[:, None] / (upper[None, :] * differ) * (1.0 - eye)
    der[0, 0] = -degree * (degree + 1) / 4.0
    der[degree, degree] = degree * (degree + 1) / 4.0
    return der, rho


def two_parts(table):
    high = np.asarray(table, np.float32).astype(jnp.bfloat16)
    low = (table - high.astype(np.float64)).astype(jnp.bfloat16)
    return high, low


def tables():
    der, rho = gll_tables()
    eye8, eye2 = np.eye(8), np.eye(2)
    plane = np.tile(np.kron(rho, rho), 2)
    fwd = np.concatenate(
        [np.kron(np.eye(16), der.T) * plane, np.kron(eye2, np.kron(der.T, eye8)) * plane], 1
    )
    high, low = two_parts(fwd)
    fwd_op = np.concatenate([high, high, low], 0)
    bwd = np.concatenate([np.kron(np.eye(16), der), np.kron(eye2, np.kron(der, eye8))], 0)
    high, low = two_parts(bwd)
    half = np.concatenate([high, low], 1)
    bwd_op = np.concatenate([half, half], 0)
    l2 = (np.arange(SUB) // EY)[:, None]
    h = (np.arange(LANES) // 64)[None, :]
    cube_plane = plane[None, :]
    zf = np.zeros((2, 2, 2, 2, SUB, LANES))
    zb = np.zeros((2, 2, 2, 2, SUB, LANES))
    rc = np.zeros((2, SUB, LANES))
    for lo in range(2):
        c_out = 2 * (2 * lo + l2) + h
        rc[lo] = rho[c_out]
        for li in range(2):
            for s in range(2):
                for l in range(2):
                    c_in = 2 * (2 * li + (l2 ^ s)) + (h ^ l)
                    zf[lo, l, li, s] = np.roll(der[c_out, c_in] * rho[c_out] * cube_plane, 64 * l, 1)
                    zb[lo, l, li, s] = np.roll(der[c_in, c_out], 64 * l, 1)
    consts = np.concatenate([zf.reshape(-1, SUB, LANES), zb.reshape(-1, SUB, LANES), rc], 0)
    return fwd_op, bwd_op, consts.astype(np.float32)


def roll_sub(x, by):
    return pltpu.roll(x, by % SUB, axis=x.ndim - 2)


def roll_lane(x, by):
    return pltpu.roll(x, by % LANES, axis=x.ndim - 1)


def split(x):
    high = x.astype(jnp.bfloat16)
    return high, (x - high.astype(jnp.float32)).astype(jnp.bfloat16)


def iotas():
    sub = lax.broadcasted_iota(jnp.int32, (SUB, LANES), 0)
    lane = lax.broadcasted_iota(jnp.int32, (SUB, LANES), 1)
    return sub, lane


def lane_gather(x, index):
    return jnp.take_along_axis(x, index, axis=1, mode="promise_in_bounds")


def flip(x, sub, lane):
    y = lane_gather(x, lane ^ 7)
    y = jnp.where(sub % 2 == 0, roll_sub(y, -1), roll_sub(y, 1))
    return jnp.where(sub % EY < 2, roll_sub(y, -2), roll_sub(y, 2))


def sum_of(parts):
    return (parts[0] + parts[1]) + (parts[2] + parts[3])


def apply_z(pair, consts, base):
    terms = []
    for v in pair:
        terms += [v, roll_sub(v, 4)]
    out = []
    for lo in range(2):
        near, far = (
            sum_of([consts[base + 8 * lo + 4 * half + t] * terms[t] for t in range(4)])
            for half in range(2)
        )
        out.append(near + roll_lane(far, 64))
    return out


def local_work(sb, u, m, fwd, bwd, consts, put_w):
    rows = sb * 64
    high, low = split(u)
    g = jnp.dot(jnp.concatenate([high, low, high], 1), fwd, preferred_element_type=jnp.float32)
    m = m.reshape(sb * EZ, 3, 16, LANES)
    gx = g[:, :LANES].reshape(sb * EZ, 16, LANES)
    gy = g[:, LANES:].reshape(sb * EZ, 16, LANES)
    fx = (gx * m[:, 0]).reshape(rows, LANES)
    fy = (gy * m[:, 1]).reshape(rows, LANES)
    xh, xl = split(fx)
    yh, yl = split(fy)
    r = jnp.dot(jnp.concatenate([xh, yh, xl, yl], 1), bwd, preferred_element_type=jnp.float32)
    r = (r[:, :LANES] + r[:, LANES:]).reshape(sb * EZ, 2, SUB, LANES)
    u4 = u.reshape(sb * EZ, 2, SUB, LANES)
    mz = m[:, 2].reshape(sb * EZ, 2, SUB, LANES)
    for i in range(sb * EZ):
        gz = apply_z([u4[i, 0], u4[i, 1]], consts, 0)
        out = apply_z([gz[0] * mz[i, 0], gz[1] * mz[i, 1]], consts, 16)
        for t in range(2):
            put_w(i // EZ, 2 * (i % EZ) + t, out[t] + consts[32 + t] * r[i, t])


def join_work(sb, get_w, get_flag, put_v, put_faces):
    sub, lane = iotas()
    ey, b = sub % EY, lane // 8 % 8
    up = (b == 7) & (ey < EY - 1)
    meets = up | ((b == 0) & (ey > 0))
    swap = jnp.where(b == 7, lane - 56, jnp.where(b == 0, lane + 56, lane))
    top_mask = (sub >= 4) & (lane >= 64)
    bot_mask = (sub < 4) & (lane < 64)
    group = lane // 16 % 4
    low_half = lane < 64
    pick = (lane % 16) * 8 + 7 * (lane // 64)
    every = range(sb)
    w = [[get_w(s, k) for k in range(8)] for s in every]
    crossed = [[lane_gather(w[s][k], swap) for k in range(8)] for s in every]
    v = [
        [
            w[s][k] + jnp.where(meets, jnp.where(up, roll_sub(crossed[s][k], -1), roll_sub(crossed[s][k], 1)), 0.0)
            for k in range(8)
        ]
        for s in every
    ]
    for s in every:
        for ez in range(EZ - 1):
            below, above = v[s][2 * ez + 1], v[s][2 * ez + 2]
            mixed = roll_lane(roll_sub(jnp.where(bot_mask, above, below), 4), 64)
            v[s][2 * ez + 1] = below + jnp.where(top_mask, mixed, 0.0)
            v[s][2 * ez + 2] = above + jnp.where(bot_mask, mixed, 0.0)
    for s in every:
        for k in range(8):
            put_v(s, k, v[s][k])
    packs = []
    for s in every:
        packs.append([])
        for k in range(8):
            got = lane_gather(v[s][k], pick)
            if k % 4 == 0:
                packs[s].append(got)
            else:
                packs[s][-1] = jnp.where(group == k % 4, got, packs[s][-1])
    turned = [roll_lane(packs[s][1], 64) for s in every]
    left = [jnp.where(low_half, packs[s][0], turned[s]) for s in every]
    right = [jnp.where(low_half, turned[s], packs[s][0]) for s in every]
    flags = [get_flag(s) for s in every]
    right = [jnp.where(flags[s], flip(right[s], sub, lane), right[s]) for s in every]
    for s in every:
        put_faces(0, s, right[s])
        put_faces(1, s, left[s])
    for side, (face, low, high) in enumerate(((right, 64, 56), (left, 0, 120))):
        index = lane % 8 + jnp.where(sub < 4, low, high)
        slot = (lane // 8 + jnp.where(sub < 4, 1, 0)) % 16
        edge = lane_gather(face[0], index)
        for s in every[1:]:
            edge = jnp.where(slot == s, lane_gather(face[s], index), edge)
        put_faces(3 + side, 0, roll_sub(edge, 4))
    ends = [jnp.where(sub < 4, v[s][0], v[s][7]) for s in every]
    for s in range(0, sb, 2):
        put_faces(2, s // 2, jnp.where((sub < 4) == (lane < 64), ends[s], roll_lane(ends[s + 1], 64)))


def neighbour_places(ids_ref, sb, slabs, peers, me):
    total = slabs * peers
    sub, lane = iotas()

    def row_of(device):
        start = device * slabs
        row = jnp.broadcast_to(ids_ref[pl.ds(start // LANES, 1), :], (SUB, LANES))
        return row, lax.rem(start, LANES)

    own, at = row_of(me)
    own = lane_gather(own, lax.rem(lane, slabs) + at)
    found = []
    for step in (-1, 1):
        other, at = row_of(lax.rem(me + peers + step, peers))
        want = own + step
        want = jnp.where(want < 0, total - 1, jnp.where(want >= total, 0, want))
        hits = jnp.zeros((SUB, LANES), jnp.int32)
        for j in range(slabs // SUB):
            place = j * SUB + sub
            hits = hits + jnp.where(lane_gather(other, place + at) == want, place, 0)
        for by in (4, 2, 1):
            hits = hits + roll_sub(hits, by)
        found += [hits, lax.div(hits, sb), lax.rem(LANES + 32 * (1 - step) - 8 * lax.rem(hits, sb), LANES)]
    table = found[0]
    for row in range(1, 6):
        table = jnp.where(sub == row, found[row], table)
    return table


def kernel(
    sb, blocks, peers, u_hbm, m_hbm, fm_hbm, ids_hbm, fwd_hbm, bwd_hbm, con_hbm, out_ref,
    u_buf, m_buf, fm_buf, ids_buf, fwd_buf, bwd_buf, con_buf, w_buf, place_buf, place, *refs
):
    sending, landing, (in_sem, once_sem, send_sem, recv_sem) = refs[:5], refs[5:10], refs[10:]
    slabs = sb * blocks
    me, layer = lax.axis_index("slab"), lax.axis_index("layer")
    right, left = lax.rem(me + 1, peers), lax.rem(me + peers - 1, peers)
    targets = (
        {"slab": right, "layer": layer},
        {"slab": left, "layer": layer},
        {"slab": me, "layer": 1 - layer},
        {"slab": right, "layer": 1 - layer},
        {"slab": left, "layer": 1 - layer},
    )
    sizes = (sb, sb, sb // 2, 1, 1)
    barrier = pltpu.get_barrier_semaphore()
    for target in targets:
        pl.semaphore_signal(barrier, inc=1, device_id=target, device_id_type=pl.DeviceIdType.MESH)

    def load_of(which, at):
        hbm, buf, size = ((u_hbm, u_buf, sb * 64), (m_hbm, m_buf, sb * 192))[which]
        rows = pl.ds(pl.multiple_of(at * size, size), size)
        return pltpu.make_async_copy(hbm.at[rows], buf.at[rows], in_sem.at[which, at])

    once = [
        pltpu.make_async_copy(src, dst, once_sem.at[n])
        for n, (src, dst) in enumerate(
            (
                (ids_hbm, ids_buf),
                (fwd_hbm, fwd_buf),
                (bwd_hbm, bwd_buf),
                (con_hbm, con_buf),
                (fm_hbm.at[:, pl.ds(0, LANES)], fm_buf),
            )
        )
    ]
    for copy in once:
        copy.start()
    for at in range(min(DEPTH, blocks)):
        load_of(0, at).start()
        load_of(1, at).start()

    def copy_of(which, at):
        rows = pl.ds(at * sizes[which], sizes[which])
        return pltpu.make_async_remote_copy(
            src_ref=sending[which].at[rows],
            dst_ref=landing[which].at[rows],
            send_sem=send_sem.at[which, at],
            recv_sem=recv_sem.at[which, at],
            device_id=targets[which],
            device_id_type=pl.DeviceIdType.MESH,
        )

    once[0].wait()
    place_buf[...] = neighbour_places(ids_buf, sb, slabs, peers, me)
    for copy in once[1:]:
        copy.wait()
    place_copy = pltpu.make_async_copy(place_buf, place, once_sem.at[len(once)])
    place_copy.start()

    def step(i, carry):
        @pl.when(i < blocks)
        def _():
            load_of(0, i).wait()
            load_of(1, i).wait()

        @pl.when(i + DEPTH < blocks)
        def _():
            load_of(0, i + DEPTH).start()
            load_of(1, i + DEPTH).start()

        @pl.when(i == 2)
        def _():
            pl.semaphore_wait(barrier, 5)

        @pl.when(i >= 2)
        def _():
            for which in range(5):
                copy_of(which, i - 2).start()

        now, last = jnp.minimum(i, blocks - 1), jnp.maximum(i - 1, 0)

        def get_w(s, k):
            return w_buf[pl.ds(s * 64 + k * 8, 8), :]

        def get_flag(s):
            return jnp.full((SUB, LANES), fm_buf[last * sb + s, 0]) != 0

        def put_v(s, k, value):
            out_ref[pl.ds(pl.multiple_of(last * sb * 64 + s * 64 + k * 8, 8), 8), :] = value

        def put_faces(which, s, value):
            sending[which][last * sizes[which] + s] = value

        def put_w(s, k, value):
            w_buf[pl.ds(s * 64 + k * 8, 8), :] = value

        @pl.when(i > 0)
        def _():
            join_work(sb, get_w, get_flag, put_v, put_faces)
        local_work(
            sb,
            u_buf[pl.ds(pl.multiple_of(now * sb * 64, sb * 64), sb * 64), :],
            m_buf[pl.ds(pl.multiple_of(now * sb * 192, sb * 192), sb * 192), :],
            fwd_buf[...],
            bwd_buf[...],
            con_buf,
            put_w,
        )
        return carry

    lax.fori_loop(0, blocks + 1, step, 0)
    for which in range(5):
        copy_of(which, blocks - 1).start()
    place_copy.wait()

    def collect(at, carry):
        for which in range(5):
            copy_of(which, at).wait_recv()
        return carry

    lax.fori_loop(0, blocks, collect, 0)

    sub, lane = iotas()
    a = lane % 8
    top_mask = (sub >= 4) & (lane >= 64)
    bot_mask = (sub < 4) & (lane < 64)
    low_half = lane < 64
    on_face = (a == 0) | (a == 7)
    spread = (lane // 8 + 64 * (a == 0).astype(jnp.int32), lane // 8 + 64 * (a == 7).astype(jnp.int32))
    edge_behind = ((sub < 4) & (lane // 8 == 8)) | ((sub >= 4) & (lane // 8 == 7))
    edge_ahead = ((sub < 4) & (lane // 8 == 0)) | ((sub >= 4) & (lane // 8 == 15))

    def with_edge(face_ref, edge_ref, row, s, mask):
        edge = pltpu.roll(edge_ref[place[row + 1, s]], place[row + 2, s], axis=1)
        return face_ref[place[row, s]] + jnp.where(mask, edge, 0.0)

    def finish(g, carry):
        every = range(GROUP)
        behind, ahead = [], []
        for n in every:
            s = g * GROUP + n
            behind.append(with_edge(landing[0], landing[3], 0, s, edge_behind))
            ahead.append(with_edge(landing[1], landing[4], 3, s, edge_ahead))
        flipped = [flip(ahead[n], sub, lane) for n in every]
        packs = []
        for n in every:
            flag = jnp.full((SUB, LANES), fm_buf[g * GROUP + n, 0]) != 0
            near = jnp.where(flag, flipped[n], ahead[n])
            packs.append((jnp.where(low_half, near, behind[n]), jnp.where(low_half, behind[n], near)))
        for k in range(8):
            index = spread[k // 4] + 16 * (k % 4)
            for n in every:
                rows = pl.ds(pl.multiple_of((g * GROUP + n) * 64 + k * 8, 8), 8)
                w = out_ref[rows, :] + jnp.where(on_face, lane_gather(packs[n][k // 4], index), 0.0)
                if k == 0 or k == 7:
                    z = roll_sub(landing[2][g * (GROUP // 2) + n // 2], 4)
                    z = z if n % 2 else roll_lane(z, 64)
                    w = w + jnp.where(bot_mask if k == 0 else top_mask, z, 0.0)
                out_ref[rows, :] = w
        return carry

    lax.fori_loop(0, slabs // GROUP, finish, 0)

    def drain(at, carry):
        for which in range(5):
            copy_of(which, at).wait_send()
        return carry

    lax.fori_loop(0, blocks, drain, 0)


def body(sb, peers, nodal_field, metric, slab_ids, face_map):
    slabs = nodal_field.shape[1]
    blocks = slabs // sb
    fwd_op, bwd_op, consts = tables()
    u = nodal_field.reshape(slabs, EZ, EY, 4, LANES).transpose(0, 1, 3, 2, 4).reshape(slabs * 64, LANES)
    m = (
        metric.reshape(slabs, EZ, EY, 3, 4, LANES)
        .transpose(0, 1, 3, 4, 2, 5)
        .reshape(slabs * 192, LANES)
    )
    ids = slab_ids.reshape(-1, LANES)
    f32 = jnp.float32
    counts = (slabs, slabs, slabs // 2, blocks, blocks)
    hbm = pl.BlockSpec(memory_space=pltpu.HBM)
    out = pl.pallas_call(
        functools.partial(kernel, sb, blocks, peers),
        in_specs=[hbm] * 7,
        out_specs=pl.BlockSpec(memory_space=pltpu.VMEM),
        out_shape=pltpu.VMEM((slabs * 64, LANES), f32),
        scratch_shapes=[
            pltpu.VMEM(u.shape, f32),
            pltpu.VMEM(m.shape, f32),
            pltpu.SMEM((slabs, LANES), jnp.int32),
            pltpu.VMEM(ids.shape, jnp.int32),
            pltpu.VMEM(fwd_op.shape, jnp.bfloat16),
            pltpu.VMEM(bwd_op.shape, jnp.bfloat16),
            pltpu.VMEM(consts.shape, f32),
            pltpu.VMEM((sb * 64, LANES), f32),
            pltpu.VMEM((SUB, LANES), jnp.int32),
            pltpu.SMEM((SUB, LANES), jnp.int32),
            *[pltpu.VMEM((n, SUB, LANES), f32) for n in counts],
            *[pltpu.VMEM((n, SUB, LANES), f32) for n in counts],
            pltpu.SemaphoreType.DMA((2, blocks)),
            pltpu.SemaphoreType.DMA((6,)),
            pltpu.SemaphoreType.DMA((5, blocks)),
            pltpu.SemaphoreType.DMA((5, blocks)),
        ],
        compiler_params=pltpu.CompilerParams(
            collective_id=0, has_side_effects=True, vmem_limit_bytes=40 * 2**20
        ),
        name="apply",
    )(
        *(
            pltpu.with_memory_space_constraint(x, pltpu.HBM)
            for x in (u, m, face_map, ids, jnp.asarray(fwd_op), jnp.asarray(bwd_op), jnp.asarray(consts))
        )
    )
    out = out.reshape(slabs, EZ, 4, EY, LANES).transpose(0, 1, 3, 2, 4)
    return out.reshape(1, slabs, EZ, EY, PTS)


def solution(mesh):
    return jax.shard_map(
        functools.partial(body, SB, mesh.shape["slab"]),
        mesh=mesh,
        in_specs=(
            P("layer", "slab", None, None, None),
            P("layer", "slab", None, None, None, None),
            P(),
            P("slab", None),
        ),
        out_specs=P("layer", "slab", None, None, None),
        check_vma=False,
    )
```

time: 28.2 us -> 25 us (0.89)
  Pallas kernels: 27.9 us -> 23.5 us
  local copies, waits for them, and re-layouts: 0 us -> 1.32 us
    pallas_call x2 -> x1, Pallas kernels: 27.9 us -> 23.5 us  [body(): pl.pallas_call(functools.partial(kernel, sb, blocks, peers), in_specs=[hb...]
    unnamed x0 -> x1, local copies, waits for them, and re-layouts: none -> 1.32 us
where the time goes in v1:
time: 25 us; the launch traced here: 24.9 us
  Pallas kernels  23.5 us (94%)
  local copies, waits for them, and re-layouts  1.32 us (5%)
    pallas_call x1, Pallas kernels, body(): pl.pallas_call(functools.partial(kernel, sb, blocks, peers), in_specs=[hb...  23.5 us
    unnamed x1, local copies, waits for them, and re-layouts  1.32 us

profile of v1, /device:TPU:0, one launch (start us, length us, event | category | flops | bytes accessed | tf_op | source)
XLA Modules:
  0.0 24.9 jit_solution(6102685447240586676)
XLA Ops:
  0.0 23.5 %apply.1 = f32[4096,128]{1,0:T(8,128)S(1)} custom-call(f32[4096,128]{1,0:T(8,128)} %bitcast.18, f32[12288,128]{1,0:T(8,128)} %bitcast.17, s32[64,1024]{1,0:T(8,128)} %fm_hbm.1, s32[8,128]{1,0:T(8,128)} %bitcast.19, bf16[384,256]{1,0:T(8,128)(2,1)} %constant.6.clone.fwd_hbm, bf16[512,256]{1,0:T(8,128)(2,1)} %constant.7.clone.bwd_hbm, ...), custom_call_target="tpu_custom_call" | custom-call | tf_op jit(solution)/shard_map/apply/pallas_call | solution.py:428
  23.5 1.3 %copy.12 = f32[1,64,4,4,512]{4,3,2,1,0:T(4,128)} copy(f32[1,64,4,4,512]{4,3,2,1,0:T(4,128)S(1)} %bitcast.16) | data formatting | bytes 4194304

commit v2 on v1

--- a/solution.py
+++ b/solution.py
@@ -16,7 +16,7 @@
 LANES = 128
 SB = 8
 DEPTH = 3
-GROUP = 16
+GROUP = 64
 
 
 def legendre_pair(nodes, degree):
@@ -64,19 +64,19 @@
     bwd_op = np.concatenate([half, half], 0)
     l2 = (np.arange(SUB) // EY)[:, None]
     h = (np.arange(LANES) // 64)[None, :]
-    cube_plane = plane[None, :]
-    zf = np.zeros((2, 2, 2, 2, SUB, LANES))
-    zb = np.zeros((2, 2, 2, 2, SUB, LANES))
-    rc = np.zeros((2, SUB, LANES))
-    for lo in range(2):
-        c_out = 2 * (2 * lo + l2) + h
-        rc[lo] = rho[c_out]
-        for li in range(2):
-            for s in range(2):
-                for l in range(2):
-                    c_in = 2 * (2 * li + (l2 ^ s)) + (h ^ l)
-                    zf[lo, l, li, s] = np.roll(der[c_out, c_in] * rho[c_out] * cube_plane, 64 * l, 1)
-                    zb[lo, l, li, s] = np.roll(der[c_in, c_out], 64 * l, 1)
+    low = 2 * l2 + h
+    zf = np.zeros((2, 2, 2, SUB, LANES))
+    zb = np.zeros((2, 2, 2, SUB, LANES))
+    for l in range(2):
+        for s in range(2):
+            c_in = 2 * (l2 ^ s) + (h ^ l)
+            for odd in range(2):
+                sign = 1 - 2 * odd
+                ahead = (der[low, c_in] + sign * der[low, 7 - c_in]) / 2
+                back = (der[c_in, low] - sign * der[c_in, 7 - low]) / 2
+                zf[odd, l, s] = np.roll(ahead * rho[low] * plane[None, :], 64 * l, 1)
+                zb[odd, l, s] = np.roll(back, 64 * l, 1)
+    rc = np.stack([np.broadcast_to(rho[low], (SUB, LANES)), np.broadcast_to(rho[4 + low], (SUB, LANES))])
     consts = np.concatenate([zf.reshape(-1, SUB, LANES), zb.reshape(-1, SUB, LANES), rc], 0)
     return fwd_op, bwd_op, consts.astype(np.float32)
 
@@ -104,50 +104,50 @@
     return jnp.take_along_axis(x, index, axis=1, mode="promise_in_bounds")
 
 
-def flip(x, sub, lane):
-    y = lane_gather(x, lane ^ 7)
+def flip_sub(y, sub):
     y = jnp.where(sub % 2 == 0, roll_sub(y, -1), roll_sub(y, 1))
     return jnp.where(sub % EY < 2, roll_sub(y, -2), roll_sub(y, 2))
 
 
-def sum_of(parts):
-    return (parts[0] + parts[1]) + (parts[2] + parts[3])
-
-
-def apply_z(pair, consts, base):
-    terms = []
-    for v in pair:
-        terms += [v, roll_sub(v, 4)]
-    out = []
-    for lo in range(2):
-        near, far = (
-            sum_of([consts[base + 8 * lo + 4 * half + t] * terms[t] for t in range(4)])
-            for half in range(2)
-        )
-        out.append(near + roll_lane(far, 64))
-    return out
-
-
-def local_work(sb, u, m, fwd, bwd, consts, put_w):
+def turn(x):
+    return roll_sub(x, 4)
+
+
+def apply_z(first, last, consts, base):
+    halves = []
+    for odd, x in enumerate((first + last, first - last)):
+        y = roll_sub(x, 4)
+        at = base + 4 * odd
+        halves.append([consts[at + 2 * l] * x + consts[at + 2 * l + 1] * y for l in range(2)])
+    (even_near, even_far), (odd_near, odd_far) = halves
+    return even_near + odd_near, even_far + odd_far, odd_near - even_near, odd_far - even_far
+
+
+def forward_work(sb, u, m, fwd, put_flux):
     rows = sb * 64
     high, low = split(u)
     g = jnp.dot(jnp.concatenate([high, low, high], 1), fwd, preferred_element_type=jnp.float32)
     m = m.reshape(sb * EZ, 3, 16, LANES)
-    gx = g[:, :LANES].reshape(sb * EZ, 16, LANES)
-    gy = g[:, LANES:].reshape(sb * EZ, 16, LANES)
-    fx = (gx * m[:, 0]).reshape(rows, LANES)
-    fy = (gy * m[:, 1]).reshape(rows, LANES)
-    xh, xl = split(fx)
-    yh, yl = split(fy)
-    r = jnp.dot(jnp.concatenate([xh, yh, xl, yl], 1), bwd, preferred_element_type=jnp.float32)
+    for n in range(2):
+        part = g[:, n * LANES : (n + 1) * LANES].reshape(sb * EZ, 16, LANES)
+        high, low = split((part * m[:, n]).reshape(rows, LANES))
+        put_flux(n, high)
+        put_flux(2 + n, low)
+
+
+def backward_work(sb, flux, u, m, bwd, consts, put_w):
+    r = jnp.dot(flux, bwd, preferred_element_type=jnp.float32)
     r = (r[:, :LANES] + r[:, LANES:]).reshape(sb * EZ, 2, SUB, LANES)
     u4 = u.reshape(sb * EZ, 2, SUB, LANES)
-    mz = m[:, 2].reshape(sb * EZ, 2, SUB, LANES)
+    mz = m.reshape(sb * EZ, 3, 2, SUB, LANES)[:, 2]
     for i in range(sb * EZ):
-        gz = apply_z([u4[i, 0], u4[i, 1]], consts, 0)
-        out = apply_z([gz[0] * mz[i, 0], gz[1] * mz[i, 1]], consts, 16)
+        near, far, near_t, far_t = apply_z(u4[i, 0], turn(roll_lane(u4[i, 1], 64)), consts, 0)
+        first = (near + roll_lane(far, 64)) * mz[i, 0]
+        last = (near_t + roll_lane(far_t, 64)) * turn(roll_lane(mz[i, 1], 64))
+        near, far, near_t, far_t = apply_z(first, last, consts, 8)
+        out = (near + roll_lane(far, 64), turn(roll_lane(near_t, 64) + far_t))
         for t in range(2):
-            put_w(i // EZ, 2 * (i % EZ) + t, out[t] + consts[32 + t] * r[i, t])
+            put_w(i // EZ, 2 * (i % EZ) + t, out[t] + consts[16 + t] * r[i, t])
 
 
 def join_work(sb, get_w, get_flag, put_v, put_faces):
@@ -189,21 +189,29 @@
                 packs[s].append(got)
             else:
                 packs[s][-1] = jnp.where(group == k % 4, got, packs[s][-1])
+    flags = [get_flag(s) for s in every]
     turned = [roll_lane(packs[s][1], 64) for s in every]
-    left = [jnp.where(low_half, packs[s][0], turned[s]) for s in every]
-    right = [jnp.where(low_half, turned[s], packs[s][0]) for s in every]
-    flags = [get_flag(s) for s in every]
-    right = [jnp.where(flags[s], flip(right[s], sub, lane), right[s]) for s in every]
+    low_flip = [lane_gather(packs[s][1], lane ^ 71) for s in every]
+    high_flip = [lane_gather(packs[s][0], lane ^ 7) for s in every]
+    mixed = [jnp.where(sub < 4, packs[s][0], packs[s][1]) for s in every]
+    spot = jnp.where(sub < 4, 0, 56)
+    edge_left = [lane_gather(mixed[s], spot + lane % 8) for s in every]
+    edge_right = [lane_gather(mixed[s], spot + 64 + lane % 8) for s in every]
+    edge_flip = [lane_gather(mixed[s], spot + 71 - lane % 8) for s in every]
+    slot = (lane // 8 + jnp.where(sub < 4, 1, 0)) % 16
+    edges = [edge_left[0], None]
     for s in every:
-        put_faces(0, s, right[s])
-        put_faces(1, s, left[s])
-    for side, (face, low, high) in enumerate(((right, 64, 56), (left, 0, 120))):
-        index = lane % 8 + jnp.where(sub < 4, low, high)
-        slot = (lane // 8 + jnp.where(sub < 4, 1, 0)) % 16
-        edge = lane_gather(face[0], index)
-        for s in every[1:]:
-            edge = jnp.where(slot == s, lane_gather(face[s], index), edge)
-        put_faces(3 + side, 0, roll_sub(edge, 4))
+        put_faces(1, s, jnp.where(low_half, packs[s][0], turned[s]))
+        right = jnp.where(low_half, turned[s], packs[s][0])
+        flipped = flip_sub(jnp.where(low_half, low_flip[s], high_flip[s]), sub)
+        put_faces(0, s, jnp.where(flags[s], flipped, right))
+        edge = jnp.where(flags[s], flip_sub(edge_flip[s], sub), edge_right[s])
+        edges = [
+            jnp.where(slot == s, edge_left[s], edges[0]),
+            edge if s == 0 else jnp.where(slot == s, edge, edges[1]),
+        ]
+    put_faces(3, 0, roll_sub(edges[1], 4))
+    put_faces(4, 0, roll_sub(edges[0], 4))
     ends = [jnp.where(sub < 4, v[s][0], v[s][7]) for s in every]
     for s in range(0, sb, 2):
         put_faces(2, s // 2, jnp.where((sub < 4) == (lane < 64), ends[s], roll_lane(ends[s + 1], 64)))
@@ -240,7 +248,7 @@
 
 def kernel(
     sb, blocks, peers, u_hbm, m_hbm, fm_hbm, ids_hbm, fwd_hbm, bwd_hbm, con_hbm, out_ref,
-    u_buf, m_buf, fm_buf, ids_buf, fwd_buf, bwd_buf, con_buf, w_buf, place_buf, place, *refs
+    u_buf, m_buf, fm_buf, ids_buf, fwd_buf, bwd_buf, con_buf, w_buf, flux_buf, place_buf, place, *refs
 ):
     sending, landing, (in_sem, once_sem, send_sem, recv_sem) = refs[:5], refs[5:10], refs[10:]
     slabs = sb * blocks
@@ -255,8 +263,6 @@
     )
     sizes = (sb, sb, sb // 2, 1, 1)
     barrier = pltpu.get_barrier_semaphore()
-    for target in targets:
-        pl.semaphore_signal(barrier, inc=1, device_id=target, device_id_type=pl.DeviceIdType.MESH)
 
     def load_of(which, at):
         hbm, buf, size = ((u_hbm, u_buf, sb * 64), (m_hbm, m_buf, sb * 192))[which]
@@ -267,19 +273,24 @@
         pltpu.make_async_copy(src, dst, once_sem.at[n])
         for n, (src, dst) in enumerate(
             (
-                (ids_hbm, ids_buf),
                 (fwd_hbm, fwd_buf),
                 (bwd_hbm, bwd_buf),
                 (con_hbm, con_buf),
                 (fm_hbm.at[:, pl.ds(0, LANES)], fm_buf),
+                (ids_hbm, ids_buf),
             )
         )
     ]
-    for copy in once:
+    once[0].start()
+    load_of(0, 0).start()
+    load_of(1, 0).start()
+    for copy in once[1:]:
         copy.start()
-    for at in range(min(DEPTH, blocks)):
+    for at in range(1, min(DEPTH, blocks)):
         load_of(0, at).start()
         load_of(1, at).start()
+    for target in targets:
+        pl.semaphore_signal(barrier, inc=1, device_id=target, device_id_type=pl.DeviceIdType.MESH)
 
     def copy_of(which, at):
         rows = pl.ds(at * sizes[which], sizes[which])
@@ -293,11 +304,6 @@
         )
 
     once[0].wait()
-    place_buf[...] = neighbour_places(ids_buf, sb, slabs, peers, me)
-    for copy in once[1:]:
-        copy.wait()
-    place_copy = pltpu.make_async_copy(place_buf, place, once_sem.at[len(once)])
-    place_copy.start()
 
     def step(i, carry):
         @pl.when(i < blocks)
@@ -310,6 +316,11 @@
             load_of(0, i + DEPTH).start()
             load_of(1, i + DEPTH).start()
 
+        @pl.when(i == 1)
+        def _():
+            for copy in once[1:4]:
+                copy.wait()
+
         @pl.when(i == 2)
         def _():
             pl.semaphore_wait(barrier, 5)
@@ -336,23 +347,48 @@
         def put_w(s, k, value):
             w_buf[pl.ds(s * 64 + k * 8, 8), :] = value
 
-        @pl.when(i > 0)
+        def fields(at):
+            return (
+                u_buf[pl.ds(pl.multiple_of(at * sb * 64, sb * 64), sb * 64), :],
+                m_buf[pl.ds(pl.multiple_of(at * sb * 192, sb * 192), sb * 192), :],
+            )
+
+        def put_flux(n, value):
+            flux_buf[n] = value
+
+        def backward():
+            flux = jnp.concatenate([flux_buf[n] for n in range(4)], 1)
+            backward_work(sb, flux, *fields(last), bwd_buf[...], con_buf, put_w)
+
+        def forward():
+            forward_work(sb, *fields(now), fwd_buf[...], put_flux)
+
+        @pl.when(i == 0)
+        def _():
+            forward()
+
+        @pl.when((i > 0) & (i < blocks))
+        def _():
+            backward()
+            forward()
+
+        @pl.when(i == blocks)
+        def _():
+            backward()
+
+        @pl.when(i >= 1)
         def _():
             join_work(sb, get_w, get_flag, put_v, put_faces)
-        local_work(
-            sb,
-            u_buf[pl.ds(pl.multiple_of(now * sb * 64, sb * 64), sb * 64), :],
-            m_buf[pl.ds(pl.multiple_of(now * sb * 192, sb * 192), sb * 192), :],
-            fwd_buf[...],
-            bwd_buf[...],
-            con_buf,
-            put_w,
-        )
+
         return carry
 
     lax.fori_loop(0, blocks + 1, step, 0)
     for which in range(5):
         copy_of(which, blocks - 1).start()
+    once[4].wait()
+    place_buf[...] = neighbour_places(ids_buf, sb, slabs, peers, me)
+    place_copy = pltpu.make_async_copy(place_buf, place, once_sem.at[len(once)])
+    place_copy.start()
     place_copy.wait()
 
     def collect(at, carry):
@@ -383,7 +419,7 @@
             s = g * GROUP + n
             behind.append(with_edge(landing[0], landing[3], 0, s, edge_behind))
             ahead.append(with_edge(landing[1], landing[4], 3, s, edge_ahead))
-        flipped = [flip(ahead[n], sub, lane) for n in every]
+        flipped = [flip_sub(lane_gather(ahead[n], lane ^ 7), sub) for n in every]
         packs = []
         for n in every:
             flag = jnp.full((SUB, LANES), fm_buf[g * GROUP + n, 0]) != 0
@@ -439,6 +475,7 @@
             pltpu.VMEM(bwd_op.shape, jnp.bfloat16),
             pltpu.VMEM(consts.shape, f32),
             pltpu.VMEM((sb * 64, LANES), f32),
+            pltpu.VMEM((4, sb * 64, LANES), jnp.bfloat16),
             pltpu.VMEM((SUB, LANES), jnp.int32),
             pltpu.SMEM((SUB, LANES), jnp.int32),
             *[pltpu.VMEM((n, SUB, LANES), f32) for n in counts],

time: 25 us -> 21 us (0.84)
  Pallas kernels: 23.5 us -> 19.5 us
    pallas_call x1, Pallas kernels: 23.5 us -> 19.5 us  [body(): pl.pallas_call(functools.partial(kernel, sb, blocks, peers), in_specs=[hb...]
where the time goes in v2:
time: 21 us; the launch traced here: 20.8 us
  Pallas kernels  19.5 us (93%)
  local copies, waits for them, and re-layouts  1.32 us (6%)
    pallas_call x1, Pallas kernels, body(): pl.pallas_call(functools.partial(kernel, sb, blocks, peers), in_specs=[hb...  19.5 us
    unnamed x1, local copies, waits for them, and re-layouts  1.32 us

profile of v2, /device:TPU:0, one launch (start us, length us, event | category | flops | bytes accessed | tf_op | source)
XLA Modules:
  0.0 20.8 jit_solution(1619524866327588132)
XLA Ops:
  0.0 19.5 %apply.1 = f32[4096,128]{1,0:T(8,128)S(1)} custom-call(f32[4096,128]{1,0:T(8,128)} %bitcast.18, f32[12288,128]{1,0:T(8,128)} %bitcast.17, s32[64,1024]{1,0:T(8,128)} %fm_hbm.1, s32[8,128]{1,0:T(8,128)} %bitcast.19, bf16[384,256]{1,0:T(8,128)(2,1)} %constant.6.clone.fwd_hbm, bf16[512,256]{1,0:T(8,128)(2,1)} %constant.7.clone.bwd_hbm, ...), custom_call_target="tpu_custom_call" | custom-call | tf_op jit(solution)/shard_map/apply/pallas_call | solution.py:464
  19.5 1.3 %copy.12 = f32[1,64,4,4,512]{4,3,2,1,0:T(4,128)} copy(f32[1,64,4,4,512]{4,3,2,1,0:T(4,128)S(1)} %bitcast.16) | data formatting | bytes 4194304

commit v3 on v2

--- a/solution.py
+++ b/solution.py
@@ -150,7 +150,7 @@
             put_w(i // EZ, 2 * (i % EZ) + t, out[t] + consts[16 + t] * r[i, t])
 
 
-def join_work(sb, get_w, get_flag, put_v, put_faces):
+def join_work(sb, first, get_w, get_flag, put_v, put_faces, put_edges):
     sub, lane = iotas()
     ey, b = sub % EY, lane // 8 % 8
     up = (b == 7) & (ey < EY - 1)
@@ -198,7 +198,7 @@
     edge_left = [lane_gather(mixed[s], spot + lane % 8) for s in every]
     edge_right = [lane_gather(mixed[s], spot + 64 + lane % 8) for s in every]
     edge_flip = [lane_gather(mixed[s], spot + 71 - lane % 8) for s in every]
-    slot = (lane // 8 + jnp.where(sub < 4, 1, 0)) % 16
+    slot = (lane // 8 + jnp.where(sub < 4, 1, 0)) % 16 - first
     edges = [edge_left[0], None]
     for s in every:
         put_faces(1, s, jnp.where(low_half, packs[s][0], turned[s]))
@@ -210,8 +210,7 @@
             jnp.where(slot == s, edge_left[s], edges[0]),
             edge if s == 0 else jnp.where(slot == s, edge, edges[1]),
         ]
-    put_faces(3, 0, roll_sub(edges[1], 4))
-    put_faces(4, 0, roll_sub(edges[0], 4))
+    put_edges(roll_sub(edges[1], 4), roll_sub(edges[0], 4))
     ends = [jnp.where(sub < 4, v[s][0], v[s][7]) for s in every]
     for s in range(0, sb, 2):
         put_faces(2, s // 2, jnp.where((sub < 4) == (lane < 64), ends[s], roll_lane(ends[s + 1], 64)))
@@ -261,7 +260,7 @@
         {"slab": right, "layer": 1 - layer},
         {"slab": left, "layer": 1 - layer},
     )
-    sizes = (sb, sb, sb // 2, 1, 1)
+    sizes = (sb, sb, sb // 2)
     barrier = pltpu.get_barrier_semaphore()
 
     def load_of(which, at):
@@ -292,16 +291,22 @@
     for target in targets:
         pl.semaphore_signal(barrier, inc=1, device_id=target, device_id_type=pl.DeviceIdType.MESH)
 
-    def copy_of(which, at):
-        rows = pl.ds(at * sizes[which], sizes[which])
-        return pltpu.make_async_remote_copy(
-            src_ref=sending[which].at[rows],
-            dst_ref=landing[which].at[rows],
-            send_sem=send_sem.at[which, at],
-            recv_sem=recv_sem.at[which, at],
-            device_id=targets[which],
-            device_id_type=pl.DeviceIdType.MESH,
-        )
+    def copies(at, count):
+        moves = [(which, pl.ds(at * sizes[which], count * sizes[which]), at) for which in range(3)]
+        if count == 2 or at == blocks - 1:
+            pair = lax.div(at, 2)
+            moves += [(which, pl.ds(pair, 1), pair) for which in (3, 4)]
+        return [
+            pltpu.make_async_remote_copy(
+                src_ref=sending[which].at[rows],
+                dst_ref=landing[which].at[rows],
+                send_sem=send_sem.at[which, sem],
+                recv_sem=recv_sem.at[which, sem],
+                device_id=targets[which],
+                device_id_type=pl.DeviceIdType.MESH,
+            )
+            for which, rows, sem in moves
+        ]
 
     once[0].wait()
 
@@ -325,27 +330,46 @@
         def _():
             pl.semaphore_wait(barrier, 5)
 
-        @pl.when(i >= 2)
-        def _():
-            for which in range(5):
-                copy_of(which, i - 2).start()
+        @pl.when((i > 2) & (i < blocks) & (lax.rem(i, 2) == 1))
+        def _():
+            for copy in copies(i - 3, 2):
+                copy.start()
+
+        @pl.when(i == blocks)
+        def _():
+            for copy in copies(blocks - 2, 1):
+                copy.start()
 
         now, last = jnp.minimum(i, blocks - 1), jnp.maximum(i - 1, 0)
 
-        def get_w(s, k):
-            return w_buf[pl.ds(s * 64 + k * 8, 8), :]
-
-        def get_flag(s):
-            return jnp.full((SUB, LANES), fm_buf[last * sb + s, 0]) != 0
-
-        def put_v(s, k, value):
-            out_ref[pl.ds(pl.multiple_of(last * sb * 64 + s * 64 + k * 8, 8), 8), :] = value
-
-        def put_faces(which, s, value):
-            sending[which][last * sizes[which] + s] = value
+        def join(at, count):
+            def get_w(s, k):
+                row = pl.multiple_of(lax.rem(at, 2) * sb * 64 + s * 64 + k * 8, 8) if count == 1 else s * 64 + k * 8
+                return w_buf[pl.ds(row, 8), :]
+
+            def get_flag(s):
+                return jnp.full((SUB, LANES), fm_buf[at * sb + s, 0]) != 0
+
+            def put_v(s, k, value):
+                out_ref[pl.ds(pl.multiple_of(at * sb * 64 + s * 64 + k * 8, 8), 8), :] = value
+
+            def put_faces(which, s, value):
+                sending[which][at * sizes[which] + s] = value
+
+            def put_edges(*edges):
+                pair = lax.div(at, 2)
+                for which, edge in zip((3, 4), edges):
+                    if count == 1:
+                        sub, lane = iotas()
+                        slot = (lane // 8 + jnp.where(sub < 4, 0, 1)) % 16
+                        edge = jnp.where(slot // sb == lax.rem(at, 2), edge, sending[which][pair])
+                    sending[which][pair] = edge
+
+            first = 0 if count == 2 else sb * lax.rem(at, 2)
+            join_work(count * sb, first, get_w, get_flag, put_v, put_faces, put_edges)
 
         def put_w(s, k, value):
-            w_buf[pl.ds(s * 64 + k * 8, 8), :] = value
+            w_buf[pl.ds(pl.multiple_of(lax.rem(last, 2) * sb * 64 + s * 64 + k * 8, 8), 8), :] = value
 
         def fields(at):
             return (
@@ -376,27 +400,29 @@
         def _():
             backward()
 
-        @pl.when(i >= 1)
-        def _():
-            join_work(sb, get_w, get_flag, put_v, put_faces)
+        @pl.when((i > 0) & (i < blocks - 1) & (lax.rem(i, 2) == 0))
+        def _():
+            join(i - 2, 2)
+
+        @pl.when(i >= blocks - 1)
+        def _():
+            join(i - 1, 1)
 
         return carry
 
     lax.fori_loop(0, blocks + 1, step, 0)
-    for which in range(5):
-        copy_of(which, blocks - 1).start()
+    for copy in copies(blocks - 1, 1):
+        copy.start()
     once[4].wait()
-    place_buf[...] = neighbour_places(ids_buf, sb, slabs, peers, me)
+    place_buf[...] = neighbour_places(ids_buf, 2 * sb, slabs, peers, me)
     place_copy = pltpu.make_async_copy(place_buf, place, once_sem.at[len(once)])
     place_copy.start()
     place_copy.wait()
 
-    def collect(at, carry):
-        for which in range(5):
-            copy_of(which, at).wait_recv()
-        return carry
-
-    lax.fori_loop(0, blocks, collect, 0)
+    every_copy = [copy for at in range(0, blocks - 2, 2) for copy in copies(at, 2)]
+    every_copy += copies(blocks - 2, 1) + copies(blocks - 1, 1)
+    for copy in every_copy:
+        copy.wait_recv()
 
     sub, lane = iotas()
     a = lane % 8
@@ -439,12 +465,8 @@
 
     lax.fori_loop(0, slabs // GROUP, finish, 0)
 
-    def drain(at, carry):
-        for which in range(5):
-            copy_of(which, at).wait_send()
-        return carry
-
-    lax.fori_loop(0, blocks, drain, 0)
+    for copy in every_copy:
+        copy.wait_send()
 
 
 def body(sb, peers, nodal_field, metric, slab_ids, face_map):
@@ -459,7 +481,7 @@
     )
     ids = slab_ids.reshape(-1, LANES)
     f32 = jnp.float32
-    counts = (slabs, slabs, slabs // 2, blocks, blocks)
+    counts = (slabs, slabs, slabs // 2, blocks // 2, blocks // 2)
     hbm = pl.BlockSpec(memory_space=pltpu.HBM)
     out = pl.pallas_call(
         functools.partial(kernel, sb, blocks, peers),
@@ -474,7 +496,7 @@
             pltpu.VMEM(fwd_op.shape, jnp.bfloat16),
             pltpu.VMEM(bwd_op.shape, jnp.bfloat16),
             pltpu.VMEM(consts.shape, f32),
-            pltpu.VMEM((sb * 64, LANES), f32),
+            pltpu.VMEM((2 * sb * 64, LANES), f32),
             pltpu.VMEM((4, sb * 64, LANES), jnp.bfloat16),
             pltpu.VMEM((SUB, LANES), jnp.int32),
             pltpu.SMEM((SUB, LANES), jnp.int32),

time: 21 us -> 20.5 us (0.976)
  Pallas kernels: 19.5 us -> 19 us
    pallas_call x1, Pallas kernels: 19.5 us -> 19 us  [body(): pl.pallas_call(functools.partial(kernel, sb, blocks, peers), in_specs=[hb...]
where the time goes in v3:
time: 20.5 us; the launch traced here: 20.4 us
  Pallas kernels  19 us (93%)
  local copies, waits for them, and re-layouts  1.32 us (6%)
    pallas_call x1, Pallas kernels, body(): pl.pallas_call(functools.partial(kernel, sb, blocks, peers), in_specs=[hb...  19 us
    unnamed x1, local copies, waits for them, and re-layouts  1.32 us

profile of v3, /device:TPU:0, one launch (start us, length us, event | category | flops | bytes accessed | tf_op | source)
XLA Modules:
  0.0 20.4 jit_solution(11117210607374138568)
XLA Ops:
  0.0 19.0 %apply.1 = f32[4096,128]{1,0:T(8,128)S(1)} custom-call(f32[4096,128]{1,0:T(8,128)} %bitcast.18, f32[12288,128]{1,0:T(8,128)} %bitcast.17, s32[64,1024]{1,0:T(8,128)} %fm_hbm.1, s32[8,128]{1,0:T(8,128)} %bitcast.19, bf16[384,256]{1,0:T(8,128)(2,1)} %constant.6.clone.fwd_hbm, bf16[512,256]{1,0:T(8,128)(2,1)} %constant.7.clone.bwd_hbm, ...), custom_call_target="tpu_custom_call" | custom-call | tf_op jit(solution)/shard_map/apply/pallas_call | solution.py:486
  19.0 1.3 %copy.12 = f32[1,64,4,4,512]{4,3,2,1,0:T(4,128)} copy(f32[1,64,4,4,512]{4,3,2,1,0:T(4,128)S(1)} %bitcast.16) | data formatting | bytes 4194304

commit v4 on v3

--- a/solution.py
+++ b/solution.py
@@ -246,8 +246,8 @@
 
 
 def kernel(
-    sb, blocks, peers, u_hbm, m_hbm, fm_hbm, ids_hbm, fwd_hbm, bwd_hbm, con_hbm, out_ref,
-    u_buf, m_buf, fm_buf, ids_buf, fwd_buf, bwd_buf, con_buf, w_buf, flux_buf, place_buf, place, *refs
+    sb, blocks, peers, u_hbm, m_hbm, fm_hbm, ids_hbm, ops_hbm, con_hbm, out_ref,
+    u_buf, m_buf, fm_buf, ids_buf, ops_buf, con_buf, w_buf, flux_buf, both_buf, place_buf, place, *refs
 ):
     sending, landing, (in_sem, once_sem, send_sem, recv_sem) = refs[:5], refs[5:10], refs[10:]
     slabs = sb * blocks
@@ -272,8 +272,7 @@
         pltpu.make_async_copy(src, dst, once_sem.at[n])
         for n, (src, dst) in enumerate(
             (
-                (fwd_hbm, fwd_buf),
-                (bwd_hbm, bwd_buf),
+                (ops_hbm, ops_buf),
                 (con_hbm, con_buf),
                 (fm_hbm.at[:, pl.ds(0, LANES)], fm_buf),
                 (ids_hbm, ids_buf),
@@ -283,11 +282,12 @@
     once[0].start()
     load_of(0, 0).start()
     load_of(1, 0).start()
-    for copy in once[1:]:
-        copy.start()
+    once[1].start()
     for at in range(1, min(DEPTH, blocks)):
         load_of(0, at).start()
         load_of(1, at).start()
+    once[2].start()
+    once[3].start()
     for target in targets:
         pl.semaphore_signal(barrier, inc=1, device_id=target, device_id_type=pl.DeviceIdType.MESH)
 
@@ -323,11 +323,11 @@
 
         @pl.when(i == 1)
         def _():
-            for copy in once[1:4]:
-                copy.wait()
+            once[1].wait()
 
         @pl.when(i == 2)
         def _():
+            once[2].wait()
             pl.semaphore_wait(barrier, 5)
 
         @pl.when((i > 2) & (i < blocks) & (lax.rem(i, 2) == 1))
@@ -382,10 +382,10 @@
 
         def backward():
             flux = jnp.concatenate([flux_buf[n] for n in range(4)], 1)
-            backward_work(sb, flux, *fields(last), bwd_buf[...], con_buf, put_w)
+            backward_work(sb, flux, *fields(last), ops_buf[3 * LANES :], con_buf, put_w)
 
         def forward():
-            forward_work(sb, *fields(now), fwd_buf[...], put_flux)
+            forward_work(sb, *fields(now), ops_buf[: 3 * LANES], put_flux)
 
         @pl.when(i == 0)
         def _():
@@ -413,16 +413,10 @@
     lax.fori_loop(0, blocks + 1, step, 0)
     for copy in copies(blocks - 1, 1):
         copy.start()
-    once[4].wait()
+    once[3].wait()
     place_buf[...] = neighbour_places(ids_buf, 2 * sb, slabs, peers, me)
     place_copy = pltpu.make_async_copy(place_buf, place, once_sem.at[len(once)])
     place_copy.start()
-    place_copy.wait()
-
-    every_copy = [copy for at in range(0, blocks - 2, 2) for copy in copies(at, 2)]
-    every_copy += copies(blocks - 2, 1) + copies(blocks - 1, 1)
-    for copy in every_copy:
-        copy.wait_recv()
 
     sub, lane = iotas()
     a = lane % 8
@@ -434,23 +428,41 @@
     edge_behind = ((sub < 4) & (lane // 8 == 8)) | ((sub >= 4) & (lane // 8 == 7))
     edge_ahead = ((sub < 4) & (lane // 8 == 0)) | ((sub >= 4) & (lane // 8 == 15))
 
-    def with_edge(face_ref, edge_ref, row, s, mask):
-        edge = pltpu.roll(edge_ref[place[row + 1, s]], place[row + 2, s], axis=1)
-        return face_ref[place[row, s]] + jnp.where(mask, edge, 0.0)
+    def with_edge(face, edge, by, mask):
+        return face + jnp.where(mask, roll_lane(edge, by), 0.0)
+
+    def prepare(pair):
+        every = range(2 * sb)
+        at = pair * 2 * sb
+        ahead = [with_edge(landing[1][at + n], landing[4][pair], -8 * n, edge_ahead) for n in every]
+        behind = [with_edge(landing[0][at + n], landing[3][pair], 64 - 8 * n, edge_behind) for n in every]
+        flipped = [lane_gather(ahead[n], lane ^ 7) for n in every]
+        for n in every:
+            landing[0][at + n] = behind[n]
+            both_buf[2 * (at + n)] = ahead[n]
+            both_buf[2 * (at + n) + 1] = flip_sub(flipped[n], sub)
+
+    def collect(pair, carry):
+        for copy in copies(2 * pair, 2):
+            copy.wait_recv()
+        prepare(pair)
+        return carry
+
+    lax.fori_loop(0, blocks // 2 - 1, collect, 0)
+    place_copy.wait()
+    last_copies = copies(blocks - 2, 1) + copies(blocks - 1, 1)
+    for copy in last_copies:
+        copy.wait_recv()
+    prepare(blocks // 2 - 1)
 
     def finish(g, carry):
         every = range(GROUP)
-        behind, ahead = [], []
+        packs = []
         for n in every:
             s = g * GROUP + n
-            behind.append(with_edge(landing[0], landing[3], 0, s, edge_behind))
-            ahead.append(with_edge(landing[1], landing[4], 3, s, edge_ahead))
-        flipped = [flip_sub(lane_gather(ahead[n], lane ^ 7), sub) for n in every]
-        packs = []
-        for n in every:
-            flag = jnp.full((SUB, LANES), fm_buf[g * GROUP + n, 0]) != 0
-            near = jnp.where(flag, flipped[n], ahead[n])
-            packs.append((jnp.where(low_half, near, behind[n]), jnp.where(low_half, behind[n], near)))
+            behind = landing[0][place[0, s]]
+            ahead = both_buf[2 * place[3, s] + jnp.minimum(fm_buf[s, 0], 1)]
+            packs.append((jnp.where(low_half, ahead, behind), jnp.where(low_half, behind, ahead)))
         for k in range(8):
             index = spread[k // 4] + 16 * (k % 4)
             for n in every:
@@ -465,7 +477,13 @@
 
     lax.fori_loop(0, slabs // GROUP, finish, 0)
 
-    for copy in every_copy:
+    def drain(pair, carry):
+        for copy in copies(2 * pair, 2):
+            copy.wait_send()
+        return carry
+
+    lax.fori_loop(0, blocks // 2 - 1, drain, 0)
+    for copy in last_copies:
         copy.wait_send()
 
 
@@ -473,6 +491,7 @@
     slabs = nodal_field.shape[1]
     blocks = slabs // sb
     fwd_op, bwd_op, consts = tables()
+    ops = np.concatenate([fwd_op, bwd_op], 0)
     u = nodal_field.reshape(slabs, EZ, EY, 4, LANES).transpose(0, 1, 3, 2, 4).reshape(slabs * 64, LANES)
     m = (
         metric.reshape(slabs, EZ, EY, 3, 4, LANES)
@@ -485,7 +504,7 @@
     hbm = pl.BlockSpec(memory_space=pltpu.HBM)
     out = pl.pallas_call(
         functools.partial(kernel, sb, blocks, peers),
-        in_specs=[hbm] * 7,
+        in_specs=[hbm] * 6,
         out_specs=pl.BlockSpec(memory_space=pltpu.VMEM),
         out_shape=pltpu.VMEM((slabs * 64, LANES), f32),
         scratch_shapes=[
@@ -493,11 +512,11 @@
             pltpu.VMEM(m.shape, f32),
             pltpu.SMEM((slabs, LANES), jnp.int32),
             pltpu.VMEM(ids.shape, jnp.int32),
-            pltpu.VMEM(fwd_op.shape, jnp.bfloat16),
-            pltpu.VMEM(bwd_op.shape, jnp.bfloat16),
+            pltpu.VMEM(ops.shape, jnp.bfloat16),
             pltpu.VMEM(consts.shape, f32),
             pltpu.VMEM((2 * sb * 64, LANES), f32),
             pltpu.VMEM((4, sb * 64, LANES), jnp.bfloat16),
+            pltpu.VMEM((2 * slabs, SUB, LANES), f32),
             pltpu.VMEM((SUB, LANES), jnp.int32),
             pltpu.SMEM((SUB, LANES), jnp.int32),
             *[pltpu.VMEM((n, SUB, LANES), f32) for n in counts],
@@ -514,7 +533,7 @@
     )(
         *(
             pltpu.with_memory_space_constraint(x, pltpu.HBM)
-            for x in (u, m, face_map, ids, jnp.asarray(fwd_op), jnp.asarray(bwd_op), jnp.asarray(consts))
+            for x in (u, m, face_map, ids, jnp.asarray(ops), jnp.asarray(consts))
         )
     )
     out = out.reshape(slabs, EZ, 4, EY, LANES).transpose(0, 1, 3, 2, 4)

time: 20.5 us -> 20.3 us (level)
  no operation moved by 1% of the time
where the time goes in v4:
time: 20.3 us; the launch traced here: 20.2 us
  Pallas kernels  18.9 us (93%)
  local copies, waits for them, and re-layouts  1.32 us (7%)
    pallas_call x1, Pallas kernels, body(): pl.pallas_call(functools.partial(kernel, sb, blocks, peers), in_specs=[hb...  18.9 us
    unnamed x1, local copies, waits for them, and re-layouts  1.32 us

profile of v4, /device:TPU:0, one launch (start us, length us, event | category | flops | bytes accessed | tf_op | source)
XLA Modules:
  0.0 20.2 jit_solution(2075119649598396185)
XLA Ops:
  0.0 18.9 %apply.1 = f32[4096,128]{1,0:T(8,128)S(1)} custom-call(f32[4096,128]{1,0:T(8,128)} %bitcast.18, f32[12288,128]{1,0:T(8,128)} %bitcast.17, s32[64,1024]{1,0:T(8,128)} %fm_hbm.1, s32[8,128]{1,0:T(8,128)} %bitcast.19, bf16[896,256]{1,0:T(8,128)(2,1)} %constant.4.clone.ops_hbm, f32[18,8,128]{2,1,0:T(8,128)} %constant.5.clone.con_hbm), custom_call_target="tpu_custom_call" | custom-call | tf_op jit(solution)/shard_map/apply/pallas_call | solution.py:505
  18.9 1.3 %copy.11 = f32[1,64,4,4,512]{4,3,2,1,0:T(4,128)} copy(f32[1,64,4,4,512]{4,3,2,1,0:T(4,128)S(1)} %bitcast.16) | data formatting | bytes 4194304
